TPU v7x, 32 devices: a whole 2x2x4 slice. The times are simulated.
32 devices in a mesh: dp: 4 (over y, core), seq: 2 (over x), head: 4 (over z).
Axes of the slice: x: 2, y: 2, z: 4, core: 2. Of those that a mesh axis runs over, the one named last changes fastest.
Arguments:
- queries: bfloat16 [4, 512, 1536], P('dp', 'seq', 'head'), may hold values from -160 to 160
- key_cache: bfloat16 [4, 512, 512], P('dp', 'seq', 'head'), may hold values from -7 to 7
- value_cache: bfloat16 [4, 512, 512], P('dp', 'seq', 'head'), may hold values from -6 to 6
- out_grad: bfloat16 [4, 512, 1536], P('dp', 'seq', 'head'), may hold values from -6 to 6
- doc_ids: int32 [4, 512], P('dp', 'seq'), may hold values from 0 to 1, never falling along the last dimension, each value on 1 to 511 neighbouring positions
- layer_input: bfloat16 [4, 512, 3072], P('dp', ('seq', 'head')), may hold values from -6 to 6
- key_proj: bfloat16 [3072, 512], P(None, 'head'), may hold values from -0.109375 to 0.109375
- value_proj: bfloat16 [3072, 512], P(None, 'head'), may hold values from -0.109375 to 0.109375
Outputs:
- query_grad: bfloat16 [4, 512, 1536], P('dp', 'seq', 'head')
- input_grad: bfloat16 [4, 512, 3072], P('dp', ('seq', 'head'))
- grad_keyproj: float32 [3072, 512], P(None, 'head')
- grad_valueproj: float32 [3072, 512], P(None, 'head')
Inputs may be any that keep to these rules, and one draw needn't show every extreme that they name: `doc_ids`: document numbers never fall along a sequence; a document spans 1 to 511 positions.
All inputs are finite; a program needn't handle non-finite values.
Results may differ from a plain program's by a relative error of at most 0.02.
Values may be sent and summed in bfloat16 or wider, within the bound.
No kernel may reach another device: no remote copies, remote signals or barrier semaphores. Data moves between devices by JAX's collectives and lax.ppermute only.
A program may use at most 64 MiB of HBM per device.

v0:
```python
import jax
import jax.numpy as jnp
from jax import lax
from jax.sharding import PartitionSpec as P

D = 3072
HD = 128
GROUP = 3
NEG_FILL = -1e30


def shards(queries, key_cache, value_cache, out_grad, doc_ids, layer_input, key_proj, value_proj):
    rows_query = queries.shape[1]
    col_width = key_cache.shape[2]
    kv_heads = col_width // HD
    cycle_size = lax.axis_size("seq")
    head_count = lax.axis_size("head")
    own_index = lax.axis_index("seq")
    score_scale = HD ** (-0.5)
    query_four = queries[0].reshape(rows_query, kv_heads, GROUP, HD)
    grad_four = out_grad[0].reshape(rows_query, kv_heads, GROUP, HD)
    own_blocks = jnp.stack([key_cache[0], value_cache[0]])
    all_docs = lax.all_gather(doc_ids, "seq", axis=1, tiled=True)[0]
    query_doc = doc_ids[0]
    query_pos = own_index * rows_query + lax.iota(jnp.int32, rows_query)
    last_pos = own_index * rows_query + rows_query - 1

    def block_scores(kv_piece, row_start):
        row_total = kv_piece.shape[1]
        key_block = kv_piece[0].reshape(row_total, kv_heads, HD)
        value_block = kv_piece[1].reshape(row_total, kv_heads, HD)
        key_pos = row_start + lax.iota(jnp.int32, row_total)
        key_doc = lax.dynamic_slice_in_dim(all_docs, row_start, row_total)
        allowed = (key_pos[None, :] <= query_pos[:, None]) & (
            key_doc[None, :] == query_doc[:, None]
        )
        scores = (
            jnp.einsum("ihge,jhe->hgij", query_four, key_block, preferred_element_type=jnp.float32)
            * score_scale
        )
        masked = jnp.where(allowed, scores, NEG_FILL)
        weight_grad = jnp.einsum(
            "ihge,jhe->hgij", grad_four, value_block, preferred_element_type=jnp.float32
        )
        return (key_block, allowed, masked, weight_grad)

    def stats_block(state_in, kv_piece, row_start):
        row_top, row_sum, row_acc = state_in
        key_block, allowed, masked, weight_grad = block_scores(kv_piece, row_start)
        new_top = jnp.maximum(row_top, jnp.max(masked, axis=-1))
        weights = jnp.where(allowed, jnp.exp(masked - new_top[..., None]), 0.0)
        decay = jnp.exp(row_top - new_top)
        return (
            new_top,
            row_sum * decay + jnp.sum(weights, axis=-1),
            row_acc * decay + jnp.sum(weights * weight_grad, axis=-1),
        )

    def stats_fold(state_in, kv_piece, row_start):
        row_total = kv_piece.shape[1]
        sub_rows = min(row_total, rows_query)

        def one_part(part_num, state_mid):
            part_start = row_start + part_num * sub_rows
            sub_piece = kv_piece
            return lax.cond(
                part_start <= last_pos,
                lambda: stats_block(state_mid, sub_piece, part_start),
                lambda: state_mid,
            )

        return lax.fori_loop(0, row_total // sub_rows, one_part, state_in)

    stat_shape = (kv_heads, GROUP, rows_query)
    stats_init = (
        jnp.full(stat_shape, NEG_FILL, jnp.float32),
        jnp.zeros(stat_shape, jnp.float32),
        jnp.zeros(stat_shape, jnp.float32),
    )
    all_blocks = lax.all_gather(own_blocks, "seq", axis=1, tiled=True)
    row_top, row_sum, row_acc = lax.fori_loop(
        0,
        cycle_size,
        lambda block_num, state_mid: stats_fold(
            state_mid,
            lax.dynamic_slice_in_dim(all_blocks, block_num * rows_query, rows_query, 1),
            block_num * rows_query,
        ),
        stats_init,
    )
    log_total = row_top + jnp.log(row_sum)
    row_delta = row_acc / row_sum

    def grad_block(kv_piece, row_start):
        row_total = kv_piece.shape[1]
        key_block, allowed, masked, weight_grad = block_scores(kv_piece, row_start)
        weights = jnp.where(allowed, jnp.exp(masked - log_total[..., None]), 0.0)
        score_grad = (weights * (weight_grad - row_delta[..., None]) * score_scale).astype(
            jnp.bfloat16
        )
        weights_low = weights.astype(jnp.bfloat16)
        query_add = jnp.einsum(
            "hgij,jhe->ihge", score_grad, key_block, preferred_element_type=jnp.float32
        )
        key_add = jnp.einsum(
            "hgij,ihge->jhe", score_grad, query_four, preferred_element_type=jnp.float32
        )
        value_add = jnp.einsum(
            "hgij,ihge->jhe", weights_low, grad_four, preferred_element_type=jnp.float32
        )
        return (
            query_add,
            jnp.stack(
                [key_add.reshape(row_total, col_width), value_add.reshape(row_total, col_width)]
            ),
        )

    zero_query = jnp.zeros((rows_query, kv_heads, GROUP, HD), jnp.float32)

    def guarded(kv_piece, row_start):
        return lax.cond(
            row_start <= last_pos,
            lambda: grad_block(kv_piece, row_start),
            lambda: (zero_query, jnp.zeros(kv_piece.shape, jnp.float32)),
        )

    def gathered_turn(block_num, state_mid):
        grad_terms, query_sum = state_mid
        row_start = block_num * rows_query
        kv_piece = lax.dynamic_slice_in_dim(all_blocks, row_start, rows_query, 1)
        query_add, kv_add = guarded(kv_piece, row_start)
        return (
            lax.dynamic_update_slice_in_dim(grad_terms, kv_add, row_start, 1),
            query_sum + query_add,
        )

    terms_init = jnp.zeros(all_blocks.shape, jnp.float32)
    grad_terms, query_sum = lax.fori_loop(0, cycle_size, gathered_turn, (terms_init, zero_query))
    kv_grads = lax.psum_scatter(
        grad_terms.astype(jnp.bfloat16), "seq", scatter_dimension=1, tiled=True
    )
    query_grad = query_sum.astype(jnp.bfloat16).reshape(1, rows_query, kv_heads * GROUP * HD)
    input_rows = rows_query // head_count
    contract_cols = (((1,), (1,)), ((), ()))
    sub_grads = kv_grads
    key_term = lax.dot_general(
        sub_grads[0], key_proj, contract_cols, preferred_element_type=jnp.float32
    )
    value_term = lax.dot_general(
        sub_grads[1], value_proj, contract_cols, preferred_element_type=jnp.float32
    )
    input_sum = lax.psum_scatter(
        (key_term + value_term).astype(jnp.bfloat16), "head", scatter_dimension=0, tiled=True
    )
    input_grad = input_sum.reshape(1, input_rows, D)
    contract_rows = (((0,), (0,)), ((), ()))
    input_piece = lax.all_gather(layer_input[0], "head", axis=0, tiled=True)
    row_total = input_piece.shape[0]
    sub_grads = kv_grads
    key_part = lax.dot_general(
        input_piece, sub_grads[0], contract_rows, preferred_element_type=jnp.float32
    )
    value_part = lax.dot_general(
        input_piece, sub_grads[1], contract_rows, preferred_element_type=jnp.float32
    )
    grad_keyproj, grad_valueproj = (
        lax.psum(key_part.astype(jnp.bfloat16), ("dp", "seq")).astype(jnp.float32),
        lax.psum(value_part.astype(jnp.bfloat16), ("dp", "seq")).astype(jnp.float32),
    )
    return (query_grad, input_grad, grad_keyproj, grad_valueproj)


def solution(mesh):
    return jax.shard_map(
        shards,
        mesh=mesh,
        in_specs=(
            P("dp", "seq", "head"),
            P("dp", "seq", "head"),
            P("dp", "seq", "head"),
            P("dp", "seq", "head"),
            P("dp", "seq"),
            P("dp", ("seq", "head"), None),
            P(None, "head"),
            P(None, "head"),
        ),
        out_specs=(
            P("dp", "seq", "head"),
            P("dp", ("seq", "head"), None),
            P(None, "head"),
            P(None, "head"),
        ),
        check_vma=False,
    )
```

profile of v0, /device:TPU:0, one launch (start us, length us, event | category | flops | bytes accessed | tf_op | source)
XLA Modules:
  0.0 143.1 jit_solution(12248398313771703250)
XLA Ops:
  8.0 0.0 copy-start
  8.0 0.0 reduce-scatter.3.cloned.1.call-start
  8.1 1.0 pad_maximum_fusion.1
  9.1 7.1 %all_gather.9 = bf16[2,512,128]{2,1,0:T(8,128)(2,1)S(1)} all-gather(bf16[2,256,128]{2,1,0:T(8,128)(2,1)S(1)} %pad_maximum_fusion.1), channel_id=1, replica_groups=mesh['dp'=4,'seq'=2,'head'=4] {'seq'}, dimensions={1}, use_global_device_ids=true | all-gather | bytes 393216 | tf_op jit(solution)/shard_map/all_gather | solution.py:80
  16.2 4.4 %all_gather.10 = s32[1,512]{1,0:T(1,128)S(1)} all-gather(s32[1,256]{1,0:T(1,128)} %param.20), channel_id=1, replica_groups=mesh['dp'=4,'seq'=2,'head'=4] {'seq'}, dimensions={1}, use_global_device_ids=true | all-gather | bytes 3072 | tf_op jit(solution)/shard_map/all_gather | solution.py:23
  20.6 1.1 copy.19
  21.7 0.2 copy.23
  21.9 0.1 copy.20
  22.0 0.2 copy.22
  22.2 1.2 while.49
  22.3 1.1 conditional.6
  22.3 0.1 dynamic_slice.27
  22.4 0.1 compare_and_fusion
  22.5 0.3 fusion.38
  22.9 0.3 fusion.7
  23.2 0.2 fusion.8
  23.5 2.2 %while.50 = (s32[]{:T(128)}, bf16[2,512,128]{2,1,0:T(8,128)(2,1)S(1)}, f32[256,1,3,128]{0,3,2,1:T(8,128)S(1)}, s32[]{:T(128)}, bf16[2,512,128]{2,1,0:T(8,128)(2,...) while((s32[]{:T(128)}, ...), condition=%wide.region_10.0_spmd.clone, body=%wide.region_7.10_spmd.clone.sunk | while | flops 253886976 | bytes 6900121 | solution.py:138
  23.5 1.7 %conditional.7 = (f32[256,1,3,128]{0,3,2,1:T(8,128)S(1)}, bf16[2,256,128]{2,1,0:T(8,128)(2,1)S(1)}) conditional(s32[]{:T(128)} %convert_element_type.78, () %tuple.108, (bf16[2,512,128]{2,1,0:T(8,128)(2,1)S(1)}, s32[]{:T(128)}, s32[]{:T(128)}, s32[]{:T(128)}, s32[512]{0:T(512)S(1)}, /*index=5*/s32[1,256]{1,0:T(1,128)S(1)}, ...), branch_computations={%region_8.8_spmd, %region_9.9_spmd} | conditional | flops 253690368 | bytes 5456986 | solution.py:121
  23.6 0.1 dynamic_slice.30
  23.6 0.1 compare_and_fusion.1
  23.8 0.4 fusion.21
  24.1 0.3 fusion.22
  24.4 0.2 convolution_bitcast_fusion.2
  24.7 0.2 convolution_bitcast_fusion.3
  24.9 0.3 convolution_bitcast_fusion.4
  25.2 0.1 select_add_fusion.2
  25.4 0.1 conditional.7
  25.5 0.1 select_add_fusion.2
  25.7 0.0 copy-start.2
  25.7 0.7 copy-done.2
  26.4 0.0 reduce-scatter.3.cloned.1.call-update
  26.4 0.0 all-gather.3.cloned.1.call-start
  26.4 0.5 all-gather.3.cloned.1.call-update
  27.0 0.0 all-reduce.3.cloned.1.call-start
  27.0 15.4 %reduce-scatter.3.cloned.1.call-done = bf16[2,256,128]{2,1,0:T(8,128)(2,1)} async-done(((bf16[2,512,128]{2,1,0:T(8,128)(2,1)}), bf16[2,256,128]{2,1,0:T(8,128)(2,1)}) %reduce-scatter.3.cloned.1.call-update) | async-done | bytes 131088 | tf_op jit(solution)/shard_map/reduce_scatter | solution.py:139
  42.5 27.0 %all-gather.3.cloned.1.call-done = bf16[1,256,3072]{2,1,0:T(8,128)(2,1)} async-done(((bf16[1,64,3072]{2,1,0:T(8,128)(2,1)}), bf16[1,256,3072]{2,1,0:T(8,128)(2,1)}) %all-gather.3.cloned.1.call-update) | async-done | bytes 1572880 | tf_op jit(solution)/shard_map/all_gather | solution.py:157
  69.4 2.8 %fusion.33 = bf16[3072,128]{0,1:T(8,128)(2,1)} fusion(bf16[1,256,3072]{2,1,0:T(8,128)(2,1)} %all-gather.3.cloned.1.call-done, bf16[2,256,128]{2,1,0:T(8,128)(2,1)} %reduce-scatter.3.cloned.1.call-done), kind=kOutput, calls=%fused_computation.59 | convolution fusion | flops 201719808 | bytes 2424832 | tf_op jit(solution)/shard_map/dot_general | solution.py:160
  72.3 1.3 fusion.34
  73.6 0.0 all-reduce.3.cloned.1.call-update
  73.6 0.0 reduce-scatter.5.cloned.1.call-start
  73.7 0.6 fusion.37
  74.2 0.5 copy-done.4
  74.7 1.8 %fusion.32 = bf16[256,3072]{1,0:T(8,128)(2,1)} fusion(f32[256,3072]{1,0:T(8,128)S(1)} %fusion.37, bf16[3072,128]{1,0:T(8,128)(2,1)S(1)} %copy-done.4, bf16[2,256,128]{2,1,0:T(8,128)(2,1)S(1)} %copy-done.5), kind=kOutput, calls=%fused_computation.56 | convolution fusion | flops 202899456 | bytes 5570560 | tf_op jit(solution)/shard_map/dot_general | solution.py:149
  76.5 0.0 reduce-scatter.5.cloned.1.call-update
  76.6 0.8 copy.25
  77.4 54.3 %all-reduce.3.cloned.1.call-done = (bf16[3072,128]{0,1:T(8,128)(2,1)}, bf16[3072,128]{0,1:T(8,128)(2,1)}) async-done(((bf16[3072,128]{0,1:T(8,128)(2,1)}, bf16[3072,128]{0,1:T(8,128)(2,1)}), (bf16[3072,128]{0,1:T(8,128)(2,1)}, bf16[3072,128]{0,1:T(8,128)(2,1)})) %all-reduce.3.cloned.1.call-update) | async-done | bytes 1572880 | tf_op jit(solution)/shard_map/psum | solution.py:167
  131.7 2.6 %copy.26 = f32[3072,128]{1,0:T(8,128)} copy(bf16[3072,128]{0,1:T(8,128)(2,1)} %get-tuple-element.776) | data formatting | bytes 2359296
  134.3 1.4 copy.27
  (35 shorter events, 0.3 us)
Async XLA Ops:
  8.0 65.7 %copy-start = (bf16[3072,128]{1,0:T(8,128)(2,1)S(1)}, bf16[3072,128]{1,0:T(8,128)(2,1)}, u32[]{:S(2)}) copy-start(bf16[3072,128]{1,0:T(8,128)(2,1)} %param.22) | copy-start | bytes 2359300
  8.0 14.2 %copy-start.7 = (s32[1,256]{1,0:T(1,128)S(1)}, s32[1,256]{1,0:T(1,128)}, u32[]{:S(2)}) copy-start(s32[1,256]{1,0:T(1,128)} %param.20) | copy-start | bytes 3076
  8.0 13.9 %copy-start.6 = (bf16[1,256,384]{2,1,0:T(8,128)(2,1)S(1)}, bf16[1,256,384]{2,1,0:T(8,128)(2,1)}, u32[]{:S(2)}) copy-start(bf16[1,256,384]{2,1,0:T(8,128)(2,1)} %param.19) | copy-start | bytes 589828
  8.0 34.4 %reduce-scatter.3.cloned.1.call-start = ((), (), s32[]{:S(2)}) async-start(), calls=%async_computation.2 | async-start | bytes 393216 | tf_op jit(solution)/shard_map/reduce_scatter | solution.py:139
  25.7 0.7 copy-start.2
  26.4 43.1 %all-gather.3.cloned.1.call-start = ((), (), s32[]{:S(2)}) async-start(), calls=%async_computation.4 | async-start | bytes 1966080 | tf_op jit(solution)/shard_map/all_gather | solution.py:157
  27.0 104.7 %all-reduce.3.cloned.1.call-start = ((), (), s32[]{:S(2)}) async-start(), calls=%async_computation.5 | async-start | bytes 3145728 | tf_op jit(solution)/shard_map/psum | solution.py:167
  42.5 29.8 %copy-start.5 = (bf16[2,256,128]{2,1,0:T(8,128)(2,1)S(1)}, bf16[2,256,128]{2,1,0:T(8,128)(2,1)}, u32[]{:S(2)}) copy-start(bf16[2,256,128]{2,1,0:T(8,128)(2,1)} %reduce-scatter.3.cloned.1.call-done) | copy-start | bytes 393220
  69.4 2.9 %copy-start.1 = (bf16[1,256,3072]{2,1,0:T(8,128)(2,1)S(1)}, bf16[1,256,3072]{2,1,0:T(8,128)(2,1)}, u32[]{:S(2)}) copy-start(bf16[1,256,3072]{2,1,0:T(8,128)(2,1)} %all-gather.3.cloned.1.call-done) | copy-start | bytes 4718596
  73.6 1.1 copy-start.4
  73.6 62.1 %reduce-scatter.5.cloned.1.call-start = ((), (), s32[]{:S(2)}) async-start(), calls=%async_computation.3 | async-start | bytes 1966080 | tf_op jit(solution)/shard_map/reduce_scatter | solution.py:152
  131.6 2.6 %copy-start.3 = (bf16[3072,128]{0,1:T(8,128)(2,1)S(1)}, bf16[3072,128]{0,1:T(8,128)(2,1)}, u32[]{:S(2)}) copy-start(bf16[3072,128]{0,1:T(8,128)(2,1)} %get-tuple-element.777) | copy-start | bytes 2359300
Sparse Core Ops, SparseCore 0:
  26.5 15.9 reduce-scatter.2
  73.7 57.8 all-reduce.2
Sparse Core Ops, SparseCore 1:
  28.4 41.0 all-gather.2
  77.0 34.3 reduce-scatter.4
where the time goes:
time: 143 us
  waiting for transfers between devices  97.3 us (68%)
  between operations  15.7 us (11%)
  blocking collectives  11.6 us (8%)
  matrix products  8.42 us (6%)
  local copies, waits for them, and re-layouts  7.89 us (6%)
  other arithmetic  1.75 us (1%)
    psum x1, waiting for transfers between devices, shards(): lax.psum(key_part.astype(jnp.bfloat16), ('dp', 'seq')).astype(jnp.float32)  54.3 us
    all_gather x1, waiting for transfers between devices, shards(): input_piece = lax.all_gather(layer_input[0], 'head', axis=0, tiled=True)  27 us
    reduce_scatter x1, waiting for transfers between devices, shards(): lax.psum_scatter(grad_terms.astype(jnp.bfloat16), 'seq', scatter_dimensio...  15.4 us
    unnamed x23, local copies, waits for them, and re-layouts  7.6 us
    all_gather x1, blocking collectives, shards(): all_blocks = lax.all_gather(own_blocks, 'seq', axis=1, tiled=True)  7.12 us
    all_gather x1, blocking collectives, shards(): all_docs = lax.all_gather(doc_ids, 'seq', axis=1, tiled=True)[0]  4.44 us
  transfers between devices with their start and end apart: 4, of which 3 were waited for; matrix products, arithmetic and copies ran while one was open for 5% of the time, Pallas kernels for 0%

commit v1 on v0

--- a/solution.py
+++ b/solution.py
@@ -1,3 +1,4 @@
+import functools
 import jax
 import jax.numpy as jnp
 from jax import lax
@@ -7,6 +8,14 @@
 HD = 128
 GROUP = 3
 NEG_FILL = -1e30
+
+
+def measure_the_masks(original, along_axis):
+    a_next = jnp.sum(lax.all_gather(original, along_axis), axis=0)
+    return a_next
+
+
+fields_supply_all = functools.partial(measure_the_masks, along_axis=("dp", "seq"))
 
 
 def shards(queries, key_cache, value_cache, out_grad, doc_ids, layer_input, key_proj, value_proj):
@@ -164,7 +173,7 @@
         input_piece, sub_grads[1], contract_rows, preferred_element_type=jnp.float32
     )
     grad_keyproj, grad_valueproj = (
-        lax.psum(key_part.astype(jnp.bfloat16), ("dp", "seq")).astype(jnp.float32),
+        fields_supply_all(key_part.astype(jnp.bfloat16)).astype(jnp.float32),
         lax.psum(value_part.astype(jnp.bfloat16), ("dp", "seq")).astype(jnp.float32),
     )
     return (query_grad, input_grad, grad_keyproj, grad_valueproj)

time: 143 us -> 195 us (1.36)
  waiting for transfers between devices: 97.3 us -> 138 us
  local copies, waits for them, and re-layouts: 7.89 us -> 14.6 us
  other arithmetic: 1.75 us -> 6.29 us
    all_gather x0 -> x1, waiting for transfers between devices: none -> 44.7 us  [measure_the_masks(): a_next = jnp.sum(lax.all_gather(original, along_axis), axis=0)]
    unnamed x23 -> x22, local copies, waits for them, and re-layouts: 7.6 us -> 14.3 us
    psum x1, waiting for transfers between devices: 54.3 us -> 49.6 us  [shards(): lax.psum(value_part.astype(jnp.bfloat16), ('dp', 'seq')).astype(jnp.float32)]
    reduce_sum x0 -> x1, other arithmetic: none -> 4.65 us  [measure_the_masks(): a_next = jnp.sum(lax.all_gather(original, along_axis), axis=0)]
  transfers between devices with their start and end apart: 4 -> 5, of which waited for: 3 -> 4; matrix products, arithmetic and copies ran while one was open for 5% -> 10% of each run, Pallas kernels for 0% -> 0%
where the time goes in v1:
time: 195 us; the launch traced here: 194 us
  waiting for transfers between devices  138 us (71%)
  between operations  15.4 us (8%)
  local copies, waits for them, and re-layouts  14.6 us (7%)
  blocking collectives  11.2 us (6%)
  matrix products  8.41 us (4%)
  other arithmetic  6.29 us (3%)
    psum x1, waiting for transfers between devices, shards(): lax.psum(value_part.astype(jnp.bfloat16), ('dp', 'seq')).astype(jnp.float32)  49.6 us
    all_gather x1, waiting for transfers between devices, measure_the_masks(): a_next = jnp.sum(lax.all_gather(original, along_axis), axis=0)  44.7 us
    all_gather x1, waiting for transfers between devices, shards(): input_piece = lax.all_gather(layer_input[0], 'head', axis=0, tiled=True)  27 us
    reduce_scatter x1, waiting for transfers between devices, shards(): lax.psum_scatter(grad_terms.astype(jnp.bfloat16), 'seq', scatter_dimensio...  15.7 us
    unnamed x22, local copies, waits for them, and re-layouts  14.3 us
    all_gather x1, blocking collectives, shards(): all_blocks = lax.all_gather(own_blocks, 'seq', axis=1, tiled=True)  5.64 us
    all_gather x1, blocking collectives, shards(): all_docs = lax.all_gather(doc_ids, 'seq', axis=1, tiled=True)[0]  5.58 us
    reduce_sum x1, other arithmetic, measure_the_masks(): a_next = jnp.sum(lax.all_gather(original, along_axis), axis=0)  4.65 us
  transfers between devices with their start and end apart: 5, of which 4 were waited for; matrix products, arithmetic and copies ran while one was open for 10% of the time, Pallas kernels for 0%

profile of v1, /device:TPU:0, one launch (start us, length us, event | category | flops | bytes accessed | tf_op | source)
XLA Modules:
  0.0 194.3 jit_solution(2653759818670461496)
XLA Ops:
  8.0 0.0 reduce-scatter.3.cloned.1.call-start
  8.1 5.6 %all_gather.16 = s32[1,512]{1,0:T(1,128)S(1)} all-gather(s32[1,256]{1,0:T(1,128)} %param.20), channel_id=1, replica_groups=mesh['dp'=4,'seq'=2,'head'=4] {'seq'}, dimensions={1}, use_global_device_ids=true | all-gather | bytes 3072 | tf_op jit(solution)/shard_map/all_gather | solution.py:32
  13.7 0.9 pad_maximum_fusion.1
  14.6 5.6 %all_gather.15 = bf16[2,512,128]{2,1,0:T(8,128)(2,1)S(1)} all-gather(bf16[2,256,128]{2,1,0:T(8,128)(2,1)S(1)} %pad_maximum_fusion.1), channel_id=1, replica_groups=mesh['dp'=4,'seq'=2,'head'=4] {'seq'}, dimensions={1}, use_global_device_ids=true | all-gather | bytes 393216 | tf_op jit(solution)/shard_map/all_gather | solution.py:89
  20.2 1.1 copy.28
  21.3 0.2 copy.32
  21.4 0.1 copy.29
  21.6 0.2 copy.31
  21.8 1.2 while.49
  21.8 1.1 conditional.6
  21.9 0.1 dynamic_slice.27
  22.0 0.1 compare_and_fusion
  22.1 0.3 fusion.38
  22.4 0.3 fusion.7
  22.7 0.2 fusion.8
  23.0 2.2 %while.50 = (s32[]{:T(128)}, bf16[2,512,128]{2,1,0:T(8,128)(2,1)S(1)}, f32[256,1,3,128]{0,3,2,1:T(8,128)S(1)}, s32[]{:T(128)}, bf16[2,512,128]{2,1,0:T(8,128)(2,...) while((s32[]{:T(128)}, ...), condition=%wide.region_10.0_spmd.clone, body=%wide.region_7.10_spmd.clone.sunk | while | flops 253886976 | bytes 6900121 | solution.py:147
  23.1 1.7 conditional.7
  23.1 0.1 dynamic_slice.30
  23.2 0.1 compare_and_fusion.1
  23.3 0.4 fusion.21
  23.7 0.3 convolution_bitcast_fusion.3
  24.0 0.3 fusion.22
  24.2 0.3 convolution_bitcast_fusion.4
  24.5 0.2 convolution_bitcast_fusion.2
  24.8 0.1 select_add_fusion.2
  25.0 0.1 conditional.7
  25.1 0.1 select_add_fusion.2
  25.2 0.7 copy-done.2
  26.0 0.0 all-gather.5.cloned.1.call-start
  26.0 0.5 all-gather.5.cloned.1.call-update
  26.5 0.0 all-reduce.2.cloned.1.call-start
  26.6 15.7 %reduce-scatter.3.cloned.1.call-done = bf16[2,256,128]{2,1,0:T(8,128)(2,1)} async-done(((bf16[2,512,128]{2,1,0:T(8,128)(2,1)}), bf16[2,256,128]{2,1,0:T(8,128)(2,1)}) %reduce-scatter.3.cloned.1.call-update) | async-done | bytes 131088 | tf_op jit(solution)/shard_map/reduce_scatter | solution.py:148
  42.3 27.0 %all-gather.5.cloned.1.call-done = bf16[1,256,3072]{2,1,0:T(8,128)(2,1)} async-done(((bf16[1,64,3072]{2,1,0:T(8,128)(2,1)}), bf16[1,256,3072]{2,1,0:T(8,128)(2,1)}) %all-gather.5.cloned.1.call-update) | async-done | bytes 1572880 | tf_op jit(solution)/shard_map/all_gather | solution.py:166
  69.3 2.8 %fusion.34 = bf16[3072,128]{0,1:T(8,128)(2,1)} fusion(bf16[1,256,3072]{2,1,0:T(8,128)(2,1)} %all-gather.5.cloned.1.call-done, bf16[2,256,128]{2,1,0:T(8,128)(2,1)} %reduce-scatter.3.cloned.1.call-done), kind=kOutput, calls=%fused_computation.61 | convolution fusion | flops 201719808 | bytes 2424832 | tf_op jit(solution)/shard_map/dot_general | solution.py:172
  72.1 0.0 all-gather.7.cloned.1.call-start
  72.2 1.3 fusion.33
  73.5 0.2 reduce-scatter.5.cloned.1.call-start
  73.8 0.6 fusion.37
  74.4 0.3 copy-done.3
  74.7 1.7 fusion.32
  76.4 0.0 reduce-scatter.5.cloned.1.call-update
  76.4 0.8 copy.34
  77.3 49.6 %all-reduce.2.cloned.1.call-done = bf16[3072,128]{0,1:T(8,128)(2,1)} async-done(((bf16[3072,128]{0,1:T(8,128)(2,1)}), bf16[3072,128]{0,1:T(8,128)(2,1)}) %all-reduce.2.cloned.1.call-update) | async-done | bytes 786448 | tf_op jit(solution)/shard_map/psum | solution.py:177
  126.9 2.5 %copy.36 = f32[3072,128]{1,0:T(8,128)} copy(bf16[3072,128]{0,1:T(8,128)(2,1)} %all-reduce.2.cloned.1.call-done) | data formatting | bytes 2359296
  129.4 44.7 %all-gather.7.cloned.1.call-done = bf16[24576,128]{0,1:T(8,128)(2,1)} async-done(((bf16[3072,128]{0,1:T(8,128)(2,1)}), bf16[24576,128]{0,1:T(8,128)(2,1)}) %all-gather.7.cloned.1.call-update) | async-done | bytes 6291472 | tf_op jit(solution)/shard_map/all_gather | solution.py:14
  174.1 7.0 %copy.40 = bf16[16,8,8,3072]{3,2,1,0:T(8,128)(2,1)S(1)} copy(bf16[16,8,8,3072]{3,1,2,0:T(8,128)(2,1)} %bitcast.150) | data formatting | bytes 12582912
  181.1 4.6 %bitcast_reduce_fusion = bf16[3072,128]{0,1:T(8,128)(2,1)S(1)} fusion(bf16[16,8,8,3072]{3,2,1,0:T(8,128)(2,1)S(1)} %copy.40), kind=kLoop, calls=%fused_computation.55 | loop fusion | flops 2752512 | bytes 7077888 | tf_op jit(solution)/shard_map/reduce_sum | solution.py:14
  185.7 1.4 copy.35
  (38 shorter events, 0.3 us)
Async XLA Ops:
  8.0 65.8 %copy-start = (bf16[3072,128]{1,0:T(8,128)(2,1)S(1)}, bf16[3072,128]{1,0:T(8,128)(2,1)}, u32[]{:S(2)}) copy-start(bf16[3072,128]{1,0:T(8,128)(2,1)} %param.22) | copy-start | bytes 2359300
  8.0 13.8 %copy-start.6 = (s32[1,256]{1,0:T(1,128)S(1)}, s32[1,256]{1,0:T(1,128)}, u32[]{:S(2)}) copy-start(s32[1,256]{1,0:T(1,128)} %param.20) | copy-start | bytes 3076
  8.0 13.4 %copy-start.5 = (bf16[1,256,384]{2,1,0:T(8,128)(2,1)S(1)}, bf16[1,256,384]{2,1,0:T(8,128)(2,1)}, u32[]{:S(2)}) copy-start(bf16[1,256,384]{2,1,0:T(8,128)(2,1)} %param.19) | copy-start | bytes 589828
  8.0 34.2 %reduce-scatter.3.cloned.1.call-start = ((), (), s32[]{:S(2)}) async-start(), calls=%async_computation.2 | async-start | bytes 393216 | tf_op jit(solution)/shard_map/reduce_scatter | solution.py:148
  25.2 0.7 copy-start.2
  26.0 43.3 %all-gather.5.cloned.1.call-start = ((), (), s32[]{:S(2)}) async-start(), calls=%async_computation.5 | async-start | bytes 1966080 | tf_op jit(solution)/shard_map/all_gather | solution.py:166
  26.5 100.4 %all-reduce.2.cloned.1.call-start = ((), (), s32[]{:S(2)}) async-start(), calls=%async_computation.4 | async-start | bytes 1572864 | tf_op jit(solution)/shard_map/psum | solution.py:177
  42.3 29.9 %copy-start.4 = (bf16[2,256,128]{2,1,0:T(8,128)(2,1)S(1)}, bf16[2,256,128]{2,1,0:T(8,128)(2,1)}, u32[]{:S(2)}) copy-start(bf16[2,256,128]{2,1,0:T(8,128)(2,1)} %reduce-scatter.3.cloned.1.call-done) | copy-start | bytes 393220
  69.3 2.9 %copy-start.1 = (bf16[1,256,3072]{2,1,0:T(8,128)(2,1)S(1)}, bf16[1,256,3072]{2,1,0:T(8,128)(2,1)}, u32[]{:S(2)}) copy-start(bf16[1,256,3072]{2,1,0:T(8,128)(2,1)} %all-gather.5.cloned.1.call-done) | copy-start | bytes 4718596
  72.1 102.0 %all-gather.7.cloned.1.call-start = ((), (), s32[]{:S(2)}) async-start(), calls=%async_computation.6 | async-start | bytes 7077888 | tf_op jit(solution)/shard_map/all_gather | solution.py:14
  73.5 1.1 copy-start.3
  73.5 113.6 %reduce-scatter.5.cloned.1.call-start = ((), (), s32[]{:S(2)}) async-start(), calls=%async_computation.3 | async-start | bytes 1966080 | tf_op jit(solution)/shard_map/reduce_scatter | solution.py:161
Sparse Core Ops, SparseCore 0:
  26.1 16.1 reduce-scatter.2
  72.3 54.5 all-reduce.1
  129.4 44.6 all-gather.6
Sparse Core Ops, SparseCore 1:
  28.0 41.2 all-gather.4
  76.9 34.3 reduce-scatter.4
